TPU v7x, 256 devices: a whole 4x4x8 slice. The times are simulated.
256 devices in a mesh: shift: 4 (over x), fsdp: 32 (over z, y_lo, core), tp: 2 (over y_hi).
Axes of the slice: x: 4, y: 4 (y_hi: 2, y_lo: 2; y = y_hi * 2 + y_lo), z: 8, core: 2. Of those that a mesh axis runs over, the one named last changes fastest.
Arguments:
- grad_stack: float32 [512, 128, 2048], P('shift', 'fsdp', 'tp'), parts along dimension 0, may hold values from -6 to 6
- moment_stack: float32 [512, 128, 2048], P('shift', 'fsdp', 'tp'), parts along dimension 0, may hold values from -6 to 6
- weight_stack: float32 [512, 128, 2048], P('shift', 'fsdp', 'tp'), parts along dimension 0, may hold values from -0.1875 to 0.1875
Outputs:
- new_weights: float32 [512, 128, 2048], P('shift', 'fsdp', 'tp'), parts along dimension 0
- new_momentum: float32 [512, 128, 2048], P('shift', 'fsdp', 'tp'), parts along dimension 0
There are 4 independent parts, one for each index of `shift`. A program takes and returns all parts, laid end to end along the dimension named above; each array names one. Nothing has to cross between parts.
All inputs are finite; a program needn't handle non-finite values.
Results may differ from a plain program's by a relative error of at most 0.0003.
Values sent between devices are 32-bit elements.
A program may use at most 64 MiB of HBM per device.

v0:
```python
import jax
import jax.numpy as jnp
from jax import lax
from jax.sharding import PartitionSpec as P

ITERS = 3


hold_rate = 0.95
learn_rate = 0.9


def gathered_total(array, axis):
    return lax.all_gather(array, axis).sum(0)


def body(grad_stack, moment_stack, weight_stack):
    new_momentum = hold_rate * moment_stack + grad_stack
    moved = lax.all_to_all(new_momentum, "fsdp", split_axis=0, concat_axis=1, tiled=True)
    total = gathered_total(jnp.sum(moved * moved, axis=(1, 2), keepdims=True), "tp")
    iterate = moved * lax.rsqrt(total + 1e-06)
    for step in range(ITERS):
        gram = gathered_total(
            jnp.einsum("mik,mjk->mij", iterate, iterate, precision=lax.Precision.HIGHEST), "tp"
        )
        mixed = -4.775 * gram + 2.0315 * jnp.einsum(
            "mij,mjk->mik", gram, gram, precision=lax.Precision.HIGHEST
        )
        iterate = 3.4445 * iterate + jnp.einsum(
            "mij,mjk->mik", mixed, iterate, precision=lax.Precision.HIGHEST
        )
    back = lax.all_to_all(iterate, "fsdp", split_axis=1, concat_axis=0, tiled=True)
    new_weights = weight_stack - learn_rate * back
    return (new_weights, new_momentum)


def solution(mesh):
    in_specs = (P("shift", "fsdp", "tp"), P("shift", "fsdp", "tp"), P("shift", "fsdp", "tp"))
    out_specs = (P("shift", "fsdp", "tp"), P("shift", "fsdp", "tp"))
    return jax.shard_map(body, mesh=mesh, in_specs=in_specs, out_specs=out_specs, check_vma=False)
```

profile of v0, /device:TPU:32, one launch (start us, length us, event | category | flops | bytes accessed | tf_op | source)
XLA Modules:
  0.0 184.6 jit_solution(4581866831942809648)
XLA Ops:
  0.6 4.6 %multiply_add_fusion.3 = f32[128,4,1024]{2,1,0:T(4,128)} fusion(f32[128,4,1024]{2,1,0:T(4,128)} %param.3, f32[128,4,1024]{2,1,0:T(4,128)} %param.4), kind=kLoop, calls=%fused_computation.6 | loop fusion | flops 1048576 | bytes 6291456 | tf_op jit(solution)/shard_map/add | solution.py:18
  5.2 0.0 copy-start.3
  5.2 9.9 %all-to-all-start = ((f32[128,4,1024]{2,1,0:T(4,128)}), f32[128,4,1024]{2,1,0:T(4,128)S(1)}, u32[]{:S(2)}, u32[]{:S(2)}) async-start(f32[128,4,1024]{2,1,0:T(4,128)} %multiply_add_fusion.3), calls=%async_computation | async-start | bytes 4194304 | tf_op jit(solution)/shard_map/all_to_all | solution.py:19
  15.1 0.0 copy-done.3
  15.1 0.6 dynamic-slice
  16.3 49.0 %all-to-all-done = f32[128,4,1024]{2,1,0:T(4,128)S(1)} async-done(((f32[128,4,1024]{2,1,0:T(4,128)}), f32[128,4,1024]{2,1,0:T(4,128)S(1)}, u32[]{:S(2)}, u32[]{:S(2)}) %all-to-all-start) | async-done | bytes 2097184 | tf_op jit(solution)/shard_map/all_to_all | solution.py:19
  65.3 0.6 multiply_reduce_fusion
  65.9 0.2 dynamic-update-slice
  66.1 6.4 %all-reduce = f32[8]{0:T(128)S(1)} all-reduce(f32[8]{0:T(128)S(1)} %dynamic-update-slice), channel_id=2, replica_groups=mesh['shift'=4,'fsdp'=32,'tp'=2] {'tp'}, use_global_device_ids=true, to_apply=%add | all-reduce | flops 8 | bytes 64
  72.5 0.1 reshape.15
  72.6 1.5 copy_bitcast_fusion
  74.2 2.0 %all_to_all.23 = f32[4,128,1024]{2,1,0:T(8,128)S(1)} reshape(f32[4,32,4,1024]{3,2,1,0:T(4,128)} %copy_bitcast_fusion) | data formatting | bytes 4194304 | tf_op jit(solution)/shard_map/all_to_all | solution.py:19
  76.2 0.0 copy-start.1
  76.2 2.3 %fusion.2 = f32[4,128,128]{2,1,0:T(8,128)S(1)} fusion(f32[4,128,1024]{2,1,0:T(8,128)S(1)} %all_to_all.23, f32[4]{0:T(128)S(1)} %add_rsqrt_fusion), kind=kOutput, calls=%fused_computation.9 | convolution fusion | flops 805830656 | bytes 2359312 | tf_op jit(solution)/shard_map/mik,mjk->mij/dot_general | solution.py:24
  78.4 8.5 %all-gather.1 = f32[8,128,128]{2,1,0:T(8,128)S(1)} all-gather(f32[4,128,128]{2,1,0:T(8,128)S(1)} %fusion.2), channel_id=3, replica_groups=mesh['shift'=4,'fsdp'=32,'tp'=2] {'tp'}, dimensions={0}, use_global_device_ids=true | all-gather | bytes 786432 | tf_op jit(solution)/shard_map/all_gather | solution.py:14
  87.0 0.0 copy-done.1
  87.0 0.4 fusion.8
  87.4 4.3 %multiply_add_fusion.2 = f32[4,128,1024]{2,1,0:T(8,128)S(1)} fusion(f32[4,128,1024]{2,1,0:T(8,128)} %copy-done.1, f32[4,128,128]{2,1,0:T(8,128)S(1)} %fusion.8, f32[4]{0:T(128)S(1)} %add_rsqrt_fusion), kind=kOutput, calls=%fused_computation.4 | convolution fusion | flops 807403520 | bytes 4456464 | tf_op jit(solution)/shard_map/mij,mjk->mik/dot_general | solution.py:29
  91.7 2.0 %fusion.11 = f32[4,128,128]{2,1,0:T(8,128)S(1)} fusion(f32[4,128,1024]{2,1,0:T(8,128)S(1)} %multiply_add_fusion.2), kind=kOutput, calls=%fused_computation.21 | convolution fusion | flops 805306368 | bytes 2359296 | tf_op jit(solution)/shard_map/mik,mjk->mij/dot_general | solution.py:24
  93.8 8.7 %all-gather.2 = f32[8,128,128]{2,1,0:T(8,128)S(1)} all-gather(f32[4,128,128]{2,1,0:T(8,128)S(1)} %fusion.11), channel_id=4, replica_groups=mesh['shift'=4,'fsdp'=32,'tp'=2] {'tp'}, dimensions={0}, use_global_device_ids=true | all-gather | bytes 786432 | tf_op jit(solution)/shard_map/all_gather | solution.py:14
  102.5 0.4 fusion.7
  102.9 2.0 %multiply_add_fusion.1 = f32[4,128,1024]{2,1,0:T(8,128)S(1)} fusion(f32[4,128,1024]{2,1,0:T(8,128)S(1)} %multiply_add_fusion.2, f32[4,128,128]{2,1,0:T(8,128)S(1)} %fusion.7), kind=kOutput, calls=%fused_computation.3 | convolution fusion | flops 806354944 | bytes 4456448 | tf_op jit(solution)/shard_map/mij,mjk->mik/dot_general | solution.py:29
  105.0 0.0 copy-start
  105.0 2.0 %fusion.12 = f32[4,128,128]{2,1,0:T(8,128)S(1)} fusion(f32[4,128,1024]{2,1,0:T(8,128)S(1)} %multiply_add_fusion.1), kind=kOutput, calls=%fused_computation.22 | convolution fusion | flops 805306368 | bytes 2359296 | tf_op jit(solution)/shard_map/mik,mjk->mij/dot_general | solution.py:24
  107.0 0.0 copy-done
  107.0 8.5 %all-gather.3 = f32[8,128,128]{2,1,0:T(8,128)S(1)} all-gather(f32[4,128,128]{2,1,0:T(8,128)S(1)} %fusion.12), channel_id=5, replica_groups=mesh['shift'=4,'fsdp'=32,'tp'=2] {'tp'}, dimensions={0}, use_global_device_ids=true | all-gather | bytes 786432 | tf_op jit(solution)/shard_map/all_gather | solution.py:14
  115.6 0.4 fusion.6
  116.0 4.2 %multiply_add_fusion = f32[4,128,1024]{2,1,0:T(8,128)S(1)} fusion(f32[4,128,1024]{2,1,0:T(8,128)} %copy-done, f32[4,128,128]{2,1,0:T(8,128)S(1)} %fusion.6), kind=kOutput, calls=%fused_computation.2 | convolution fusion | flops 806354944 | bytes 4456448 | tf_op jit(solution)/shard_map/mij,mjk->mik/dot_general | solution.py:29
  120.2 1.4 copy.8
  121.6 58.1 %all_to_all.27 = f32[4,128,1024]{2,0,1:T(4,128)S(1)} all-to-all(f32[4,128,1024]{2,0,1:T(4,128)S(1)} %copy.8), channel_id=1, replica_groups=mesh['shift'=4,'fsdp'=32,'tp'=2] {'fsdp'}, dimensions={1} | all-to-all | bytes 4194304 | tf_op jit(solution)/shard_map/all_to_all | solution.py:32
  179.7 0.7 broadcast_multiply_fusion
  180.4 0.0 copy-start.2
  180.4 1.8 copy.9
  182.2 0.0 copy-done.2
  182.2 2.4 %bitcast_subtract_fusion = f32[128,4,1024]{2,1,0:T(4,128)} fusion(f32[128,4,1024]{2,1,0:T(4,128)S(1)} %copy-done.2, f32[32,4,4,1024]{3,2,1,0:T(4,128)S(1)} %copy.9), kind=kLoop, calls=%fused_computation | loop fusion | flops 524288 | bytes 6291456 | tf_op jit(solution)/shard_map/sub | solution.py:33
  (6 shorter events, 0.1 us)
Async XLA Ops:
  5.2 9.9 %copy-start.3 = (u32[256]{0:T(256)S(1)}, u32[256]{0:T(256)}, u32[]{:S(2)}) copy-start(u32[256]{0:T(256)} %constant.19) | copy-start | bytes 3076
  5.2 60.1 %all-to-all-start = ((f32[128,4,1024]{2,1,0:T(4,128)}), f32[128,4,1024]{2,1,0:T(4,128)S(1)}, u32[]{:S(2)}, u32[]{:S(2)}) async-start(f32[128,4,1024]{2,1,0:T(4,128)} %multiply_add_fusion.3), calls=%async_computation | async-start | bytes 4194304 | tf_op jit(solution)/shard_map/all_to_all | solution.py:19
  76.2 10.9 %copy-start.1 = (f32[4,128,1024]{2,1,0:T(8,128)}, f32[4,128,1024]{2,1,0:T(8,128)S(1)}, u32[]{:S(2)}) copy-start(f32[4,128,1024]{2,1,0:T(8,128)S(1)} %all_to_all.23) | copy-start | bytes 6291460
  105.0 2.1 %copy-start = (f32[4,128,1024]{2,1,0:T(8,128)}, f32[4,128,1024]{2,1,0:T(8,128)S(1)}, u32[]{:S(2)}) copy-start(f32[4,128,1024]{2,1,0:T(8,128)S(1)} %multiply_add_fusion.1) | copy-start | bytes 6291460
  180.4 1.8 copy-start.2
where the time goes:
time: 187 us; the launch traced here: 185 us
  blocking collectives  90.3 us (48%)
  waiting for transfers between devices  49 us (26%)
  matrix products  18 us (10%)
  starting transfers between devices  9.87 us (5%)
  other arithmetic  8.38 us (4%)
  local copies, waits for them, and re-layouts  7.56 us (4%)
    all_to_all x1, blocking collectives, body(): lax.all_to_all(iterate, 'fsdp', split_axis=1, concat_axis=0, tiled=True)  58.1 us
    all_to_all x1, waiting for transfers between devices, body(): lax.all_to_all(new_momentum, 'fsdp', split_axis=0, concat_axis=1, tiled=T...  49 us
    all_gather x3, blocking collectives, gathered_total(): return lax.all_gather(array, axis).sum(0)  25.8 us
    dot_general x3, matrix products, body(): jnp.einsum('mij,mjk->mik', mixed, iterate, precision=lax.Precision.HIGHEST)  10.6 us
    all_to_all x1, starting transfers between devices, body(): lax.all_to_all(new_momentum, 'fsdp', split_axis=0, concat_axis=1, tiled=T...  9.87 us
    unnamed x1, blocking collectives  6.41 us
    dot_general x3, matrix products, body(): jnp.einsum('mik,mjk->mij', iterate, iterate, precision=lax.Precision.HIGH...  6.35 us
    add x1, other arithmetic, body(): new_momentum = hold_rate * moment_stack + grad_stack  4.57 us
  transfers between devices with their start and end apart: 1, of which 1 were waited for; matrix products, arithmetic and copies ran while one was open for 0% of the time, Pallas kernels for 0%

commit v1 on v0

v1 whole, which is shorter than its diff:
```python
import functools

import jax
import jax.numpy as jnp
from jax import lax
from jax.experimental import pallas as pl
from jax.experimental.pallas import tpu as pltpu
from jax.sharding import PartitionSpec as P

MESH = pl.DeviceIdType.MESH
ITERS = 3
hold_rate = 0.95
learn_rate = 0.9


def full_dot(a, b, dims):
    return lax.dot_general(
        a, b, (dims, ((), ())), precision=lax.Precision.HIGHEST, preferred_element_type=jnp.float32
    )


def times(a, b):
    return full_dot(a, b, ((1,), (0,)))


def polynomial(gram):
    side = gram.shape[0]
    eye = lax.broadcasted_iota(jnp.int32, (side, side), 0) == lax.broadcasted_iota(
        jnp.int32, (side, side), 1
    )
    total = jnp.sum(jnp.sum(jnp.where(eye, gram, 0.0), axis=1, keepdims=True), axis=0, keepdims=True)
    scale = lax.rsqrt(total + 1e-06)
    a = gram * (scale * scale)
    whole = None
    for step in range(ITERS):
        mixed = -4.775 * a + 2.0315 * times(a, a)
        mixed = jnp.where(eye, mixed + 3.4445, mixed)
        whole = mixed if whole is None else times(mixed, whole)
        if step < ITERS - 1:
            a = times(times(mixed, a), mixed)
    return whole * scale


def kernel(
    group,
    waves,
    g_ref,
    m_ref,
    w_ref,
    weights,
    momentum,
    g_buf,
    m_buf,
    w_buf,
    arrived,
    leaving,
    returned,
    rows,
    gram_out,
    gram_in,
    load_sem,
    w_sem,
    out_send,
    out_recv,
    gram_send,
    gram_recv,
    back_send,
    back_recv,
):
    me, half = lax.axis_index("fsdp"), lax.axis_index("tp")
    near, other = rows.shape[0] // group, lax.rem(half + 1, 2)

    def peer(o):
        return lax.rem(me + o, group)

    barrier = pltpu.get_barrier_semaphore()

    def greet(o, _):
        pl.semaphore_signal(barrier, inc=1, device_id={"fsdp": peer(o)}, device_id_type=MESH)
        return 0

    lax.fori_loop(1, group, greet, 0)
    pl.semaphore_signal(barrier, inc=1, device_id={"tp": other}, device_id_type=MESH)

    def part(w):
        return pl.ds(w * group, group)

    def loads(w):
        return (
            pltpu.make_async_copy(g_ref.at[part(w)], g_buf.at[part(w)], load_sem.at[0, w]),
            pltpu.make_async_copy(m_ref.at[part(w)], m_buf.at[part(w)], load_sem.at[1, w]),
        )

    for w in range(waves):
        for copy in loads(w):
            copy.start()
    w_copy = pltpu.make_async_copy(w_ref, w_buf, w_sem)
    w_copy.start()

    def out_copy(w, o):
        return pltpu.make_async_remote_copy(
            src_ref=momentum.at[w * group + peer(o)],
            dst_ref=arrived.at[w, me],
            send_sem=out_send.at[w],
            recv_sem=out_recv.at[w],
            device_id={"fsdp": peer(o)},
            device_id_type=MESH,
        )

    def back_copy(w, o):
        return pltpu.make_async_remote_copy(
            src_ref=leaving.at[w, peer(o)],
            dst_ref=returned.at[w * group + me],
            send_sem=back_send.at[w],
            recv_sem=back_recv.at[w],
            device_id={"fsdp": peer(o)},
            device_id_type=MESH,
        )

    def all_of(buf, send, recv):
        return pltpu.make_async_remote_copy(
            src_ref=buf, dst_ref=buf, send_sem=send, recv_sem=recv,
            device_id={"fsdp": me}, device_id_type=MESH,
        )

    def gram_copy(w):
        return pltpu.make_async_remote_copy(
            src_ref=gram_out.at[w],
            dst_ref=gram_in.at[w],
            send_sem=gram_send.at[w],
            recv_sem=gram_recv.at[w],
            device_id={"tp": other},
            device_id_type=MESH,
        )

    for w in range(waves):
        for copy in loads(w):
            copy.wait()
        momentum[part(w)] = hold_rate * m_buf[part(w)] + g_buf[part(w)]
        if w == 0:
            pl.semaphore_wait(barrier, group)

        def send(o, _, w=w):
            out_copy(w, o).start()
            return 0

        lax.fori_loop(1, group, send, 0)
        arrived[w, me] = momentum[w * group + me]

    def wave(w, _):
        all_of(arrived.at[w, pl.ds(0, group - 1)], out_send.at[w], out_recv.at[w]).wait_recv()
        for k in range(group // 2):
            rows[pl.ds(2 * near * k, 2 * near), :] = jnp.concatenate(
                [arrived[w, 2 * k], arrived[w, 2 * k + 1]], axis=0
            )
        mat = rows[...]
        gram_out[w] = full_dot(mat, mat, ((1,), (1,)))
        gram_copy(w).start()
        gram_copy(w).wait_recv()
        mix = polynomial(gram_out[w] + gram_in[w])
        product = times(mix, rows[...])
        for k in range(group):
            leaving[w, k] = product[near * k : near * (k + 1)]

        def send(o, _):
            back_copy(w, o).start()
            return 0

        lax.fori_loop(1, group, send, 0)
        returned[w * group + me] = leaving[w, me]
        return 0

    lax.fori_loop(0, waves, wave, 0)
    w_copy.wait()

    def finish(w, _):
        all_of(returned.at[pl.ds(w * group, group - 1)], back_send.at[w], back_recv.at[w]).wait_recv()
        weights[part(w)] = w_buf[part(w)] - learn_rate * returned[part(w)]
        return 0

    lax.fori_loop(0, waves, finish, 0)

    def drain(w, _):
        all_of(arrived.at[w, pl.ds(0, group - 1)], out_send.at[w], out_recv.at[w]).wait_send()
        gram_copy(w).wait_send()
        all_of(returned.at[pl.ds(w * group, group - 1)], back_send.at[w], back_recv.at[w]).wait_send()
        return 0

    lax.fori_loop(0, waves, drain, 0)


def solution(mesh):
    group = mesh.shape["fsdp"]

    def body(g, m, w):
        mats, near, wide = g.shape
        waves, side = mats // group, near * group
        block = jax.ShapeDtypeStruct(g.shape, jnp.float32)
        f32 = jnp.float32
        sem = pltpu.SemaphoreType.DMA
        return pl.pallas_call(
            functools.partial(kernel, group, waves),
            name="update",
            out_shape=(block, block),
            in_specs=[pl.BlockSpec(memory_space=pltpu.HBM)] * 3,
            out_specs=[pl.BlockSpec(memory_space=pltpu.VMEM)] * 2,
            scratch_shapes=[
                pltpu.VMEM(g.shape, f32),
                pltpu.VMEM(g.shape, f32),
                pltpu.VMEM(g.shape, f32),
                pltpu.VMEM((waves, group, near, wide), f32),
                pltpu.VMEM((waves, group, near, wide), f32),
                pltpu.VMEM(g.shape, f32),
                pltpu.VMEM((side, wide), f32),
                pltpu.VMEM((waves, side, side), f32),
                pltpu.VMEM((waves, side, side), f32),
                sem((2, waves)),
                sem,
                sem((waves,)),
                sem((waves,)),
                sem((waves,)),
                sem((waves,)),
                sem((waves,)),
                sem((waves,)),
            ],
            compiler_params=pltpu.CompilerParams(
                collective_id=0, has_side_effects=True, vmem_limit_bytes=40 * 1024 * 1024
            ),
        )(g, m, w)

    specs = P("shift", "fsdp", "tp")
    return jax.shard_map(
        body, mesh=mesh, in_specs=(specs,) * 3, out_specs=(specs,) * 2, check_vma=False
    )
```

time: 187 us -> 113 us (0.60)
  the two profiles are of different devices: /device:TPU:32 before, /device:TPU:9 now
where the time goes in v1:
time: 113 us
  Pallas kernels  105 us (93%)
  local copies, waits for them, and re-layouts  7.41 us (7%)
    pallas_call x1, Pallas kernels, body(): pl.pallas_call(functools.partial(kernel, group, waves), name='update', ou...  105 us
    unnamed x8, local copies, waits for them, and re-layouts  7.41 us

profile of v1, /device:TPU:9, one launch (start us, length us, event | category | flops | bytes accessed | tf_op | source)
XLA Modules:
  0.0 113.0 jit_solution(1768565242842040348)
XLA Ops:
  0.6 0.0 copy-start
  0.6 1.6 %copy-done = f32[128,4,1024]{2,1,0:T(4,128)S(1)} copy-done((f32[128,4,1024]{2,1,0:T(4,128)S(1)}, f32[128,4,1024]{2,1,0:T(4,128)}, u32[]{:S(2)}) %copy-start) | copy-done | bytes 2097176
  2.2 0.0 copy-start.1
  2.2 1.6 %copy-done.1 = f32[128,4,1024]{2,1,0:T(4,128)S(1)} copy-done((f32[128,4,1024]{2,1,0:T(4,128)S(1)}, f32[128,4,1024]{2,1,0:T(4,128)}, u32[]{:S(2)}) %copy-start.1) | copy-done | bytes 2097176
  3.8 0.0 copy-start.2
  3.8 1.6 %copy-done.2 = f32[128,4,1024]{2,1,0:T(4,128)S(1)} copy-done((f32[128,4,1024]{2,1,0:T(4,128)S(1)}, f32[128,4,1024]{2,1,0:T(4,128)}, u32[]{:S(2)}) %copy-start.2) | copy-done | bytes 2097176
  5.4 104.9 %update.1 = (f32[128,4,1024]{2,1,0:T(4,128)S(1)}, f32[128,4,1024]{2,1,0:T(4,128)S(1)}) custom-call(f32[128,4,1024]{2,1,0:T(4,128)S(1)} %copy-done, f32[128,4,1024]{2,1,0:T(4,128)S(1)} %copy-done.1, f32[128,4,1024]{2,1,0:T(4,128)S(1)} %copy-done.2), custom_call_target="tpu_custom_call" | custom-call | tf_op jit(solution)/shard_map/update/pallas_call | solution.py:201
  110.3 1.3 %copy.7 = f32[128,4,1024]{2,1,0:T(4,128)} copy(f32[128,4,1024]{2,1,0:T(4,128)S(1)} %get-tuple-element.4) | data formatting | bytes 4194304
  111.6 1.3 %copy.8 = f32[128,4,1024]{2,1,0:T(4,128)} copy(f32[128,4,1024]{2,1,0:T(4,128)S(1)} %get-tuple-element.5) | data formatting | bytes 4194304
Async XLA Ops:
  0.6 1.6 %copy-start = (f32[128,4,1024]{2,1,0:T(4,128)S(1)}, f32[128,4,1024]{2,1,0:T(4,128)}, u32[]{:S(2)}) copy-start(f32[128,4,1024]{2,1,0:T(4,128)} %g_ref.1) | copy-start | bytes 6291460
  2.2 1.6 %copy-start.1 = (f32[128,4,1024]{2,1,0:T(4,128)S(1)}, f32[128,4,1024]{2,1,0:T(4,128)}, u32[]{:S(2)}) copy-start(f32[128,4,1024]{2,1,0:T(4,128)} %m_ref.1) | copy-start | bytes 6291460
  3.8 1.6 %copy-start.2 = (f32[128,4,1024]{2,1,0:T(4,128)S(1)}, f32[128,4,1024]{2,1,0:T(4,128)}, u32[]{:S(2)}) copy-start(f32[128,4,1024]{2,1,0:T(4,128)} %w_ref.1) | copy-start | bytes 6291460

commit v2 on v1

--- a/solution.py
+++ b/solution.py
@@ -224,7 +224,7 @@
                 sem((waves,)),
             ],
             compiler_params=pltpu.CompilerParams(
-                collective_id=0, has_side_effects=True, vmem_limit_bytes=40 * 1024 * 1024
+                collective_id=0, has_side_effects=True, vmem_limit_bytes=48 * 1024 * 1024
             ),
         )(g, m, w)
 

time: 113 us -> 108 us (0.956)
  the two profiles are of different devices: /device:TPU:9 before, /device:TPU:1 now
where the time goes in v2:
time: 108 us
  Pallas kernels  105 us (97%)
  local copies, waits for them, and re-layouts  2.64 us (2%)
    pallas_call x1, Pallas kernels, body(): pl.pallas_call(functools.partial(kernel, group, waves), name='update', ou...  105 us
    unnamed x2, local copies, waits for them, and re-layouts  2.64 us

profile of v2, /device:TPU:1, one launch (start us, length us, event | category | flops | bytes accessed | tf_op | source)
XLA Modules:
  0.0 108.1 jit_solution(4396377432365981574)
XLA Ops:
  0.6 104.8 %update.1 = (f32[128,4,1024]{2,1,0:T(4,128)S(1)}, f32[128,4,1024]{2,1,0:T(4,128)S(1)}) custom-call(f32[128,4,1024]{2,1,0:T(4,128)} %g_ref.1, f32[128,4,1024]{2,1,0:T(4,128)} %m_ref.1, f32[128,4,1024]{2,1,0:T(4,128)} %w_ref.1), custom_call_target="tpu_custom_call" | custom-call | tf_op jit(solution)/shard_map/update/pallas_call | solution.py:201
  105.4 1.3 %copy.7 = f32[128,4,1024]{2,1,0:T(4,128)} copy(f32[128,4,1024]{2,1,0:T(4,128)S(1)} %get-tuple-element.4) | data formatting | bytes 4194304
  106.7 1.3 %copy.8 = f32[128,4,1024]{2,1,0:T(4,128)} copy(f32[128,4,1024]{2,1,0:T(4,128)S(1)} %get-tuple-element.5) | data formatting | bytes 4194304

commit v3 on v2

v3 whole, which is shorter than its diff:
```python
import functools

import jax
import jax.numpy as jnp
from jax import lax
from jax.experimental import pallas as pl
from jax.experimental.pallas import tpu as pltpu
from jax.sharding import PartitionSpec as P

MESH = pl.DeviceIdType.MESH
MIB = 1024 * 1024
ITERS = 3
hold_rate = 0.95
learn_rate = 0.9

def order():
    plus = [(dz, b, c) for b, c in ((0, 0), (1, 1), (0, 1), (1, 0)) for dz in (3, 2, 1)]
    minus = [(dz, b, c) for b, c in ((0, 0), (1, 1), (0, 1), (1, 0)) for dz in (5, 6, 7)]
    far = [(4, b, c) for b, c in ((0, 0), (1, 1), (0, 1), (1, 0))]
    out = []
    for i, pair in enumerate(zip(plus, minus)):
        out += pair
        if i % 3 == 2:
            out.append(far[i // 3])
    return out + [(0, 1, 0), (0, 0, 1), (0, 1, 1)]


def full_dot(a, b, dims):
    return lax.dot_general(
        a, b, (dims, ((), ())), precision=lax.Precision.HIGHEST, preferred_element_type=jnp.float32
    )


def times(a, b):
    return full_dot(a, b, ((1,), (0,)))


def polynomial(gram):
    side = gram.shape[0]
    eye = lax.broadcasted_iota(jnp.int32, (side, side), 0) == lax.broadcasted_iota(
        jnp.int32, (side, side), 1
    )
    total = jnp.sum(jnp.sum(jnp.where(eye, gram, 0.0), axis=1, keepdims=True), axis=0, keepdims=True)
    scale = lax.rsqrt(total + 1e-06)
    a = gram * (scale * scale)
    whole = None
    for step in range(ITERS):
        mixed = -4.775 * a + 2.0315 * times(a, a)
        mixed = jnp.where(eye, mixed + 3.4445, mixed)
        whole = mixed if whole is None else times(mixed, whole)
        if step < ITERS - 1:
            a = times(times(mixed, a), mixed)
    return whole * scale


def exchange(
    group,
    waves,
    g_ref,
    m_ref,
    w_ref,
    weights,
    momentum,
    last,
    g_buf,
    m_buf,
    arrived,
    leaving,
    returned,
    rows,
    gram_out,
    gram_in,
    load_sem,
    w_sem,
    out_send,
    out_recv,
    gram_send,
    gram_recv,
    back_send,
    back_recv,
):
    me, half = lax.axis_index("fsdp"), lax.axis_index("tp")
    near, other = rows.shape[0] // group, lax.rem(half + 1, 2)
    z, y, core = me // 4, lax.rem(me // 2, 2), lax.rem(me, 2)
    depth = group // 4

    def partner(step):
        dz, dy, dc = step
        return lax.rem(z + dz, depth) * 4 + lax.rem(y + dy, 2) * 2 + lax.rem(core + dc, 2)

    barrier = pltpu.get_barrier_semaphore()

    def greet(o, _):
        pl.semaphore_signal(
            barrier, inc=1, device_id={"fsdp": lax.rem(me + o, group)}, device_id_type=MESH
        )
        return 0

    lax.fori_loop(1, group, greet, 0)
    pl.semaphore_signal(barrier, inc=1, device_id={"tp": other}, device_id_type=MESH)

    def part(w):
        return pl.ds(w * group, group)

    def loads(w):
        return (
            pltpu.make_async_copy(g_ref.at[part(w)], g_buf.at[part(w)], load_sem.at[0, w]),
            pltpu.make_async_copy(m_ref.at[part(w)], m_buf.at[part(w)], load_sem.at[1, w]),
        )

    for w in range(waves):
        for copy in loads(w):
            copy.start()
    w_copy = pltpu.make_async_copy(w_ref, weights, w_sem)
    w_copy.start()

    def out_copy(w, to):
        return pltpu.make_async_remote_copy(
            src_ref=momentum.at[w * group + to],
            dst_ref=arrived.at[w, me],
            send_sem=out_send.at[w],
            recv_sem=out_recv.at[w],
            device_id={"fsdp": to},
            device_id_type=MESH,
        )

    def back_copy(w, to):
        return pltpu.make_async_remote_copy(
            src_ref=leaving.at[w, to],
            dst_ref=returned.at[w, me],
            send_sem=back_send.at[w],
            recv_sem=back_recv.at[w],
            device_id={"fsdp": to},
            device_id_type=MESH,
        )

    def all_of(buf, w, send, recv):
        blocks = buf.at[w, pl.ds(0, group - 1)]
        return pltpu.make_async_remote_copy(
            src_ref=blocks, dst_ref=blocks, send_sem=send.at[w], recv_sem=recv.at[w],
            device_id={"fsdp": me}, device_id_type=MESH,
        )

    def gram_copy(w):
        return pltpu.make_async_remote_copy(
            src_ref=gram_out.at[w],
            dst_ref=gram_in.at[w],
            send_sem=gram_send.at[w],
            recv_sem=gram_recv.at[w],
            device_id={"tp": other},
            device_id_type=MESH,
        )

    for w in range(waves):
        for copy in loads(w):
            copy.wait()
        momentum[part(w)] = hold_rate * m_buf[part(w)] + g_buf[part(w)]
        arrived[w, me] = momentum[w * group + me]
    pl.semaphore_wait(barrier, group)

    def send_out(w, _):
        for step in order():
            out_copy(w, partner(step)).start()
        return 0

    lax.fori_loop(0, waves, send_out, 0)

    def wave(w, _):
        all_of(arrived, w, out_send, out_recv).wait_recv()
        for k in range(group // 2):
            rows[pl.ds(2 * near * k, 2 * near), :] = jnp.concatenate(
                [arrived[w, 2 * k], arrived[w, 2 * k + 1]], axis=0
            )
        mat = rows[...]
        gram_out[w] = full_dot(mat, mat, ((1,), (1,)))
        gram_copy(w).start()
        gram_copy(w).wait_recv()
        mix = polynomial(gram_out[w] + gram_in[w])
        product = times(mix, rows[...])
        for k in range(group):
            leaving[w, k] = product[near * k : near * (k + 1)]
        for step in order():
            back_copy(w, partner(step)).start()
        returned[w, me] = leaving[w, me]
        return 0

    lax.fori_loop(0, waves, wave, 0)
    w_copy.wait()

    def finish(w, _):
        all_of(returned, w, back_send, back_recv).wait_recv()
        weights[part(w)] = weights[part(w)] - learn_rate * returned[w]
        return 0

    lax.fori_loop(0, waves - 1, finish, 0)

    def drain(w, _):
        all_of(arrived, w, out_send, out_recv).wait_send()
        gram_copy(w).wait_send()
        all_of(returned, w, back_send, back_recv).wait_send()
        return 0

    lax.fori_loop(0, waves, drain, 0)
    all_of(returned, waves - 1, back_send, back_recv).wait_recv()
    last[...] = returned[waves - 1]


def store(weights, momentum, last, weights_out, momentum_out, fresh, sem):
    done = weights.shape[0] - last.shape[0]
    tail = pl.ds(done, last.shape[0])
    copies = [
        pltpu.make_async_copy(weights.at[pl.ds(0, done)], weights_out.at[pl.ds(0, done)], sem.at[0]),
        pltpu.make_async_copy(momentum, momentum_out, sem.at[1]),
        pltpu.make_async_copy(fresh, weights_out.at[tail], sem.at[2]),
    ]
    copies[0].start()
    copies[1].start()
    fresh[...] = weights[tail] - learn_rate * last[...]
    copies[2].start()
    for copy in copies:
        copy.wait()


def solution(mesh):
    group = mesh.shape["fsdp"]

    def body(g, m, w):
        mats, near, wide = g.shape
        waves, side = mats // group, near * group
        f32 = jnp.float32
        block = jax.ShapeDtypeStruct(g.shape, f32)
        fifth = jax.ShapeDtypeStruct((group, near, wide), f32)
        sem = pltpu.SemaphoreType.DMA
        in_hbm, in_vmem = pl.BlockSpec(memory_space=pltpu.HBM), pl.BlockSpec(memory_space=pltpu.VMEM)
        blocks = pltpu.VMEM((waves, group, near, wide), f32)
        squares = pltpu.VMEM((waves, side, side), f32)
        weights, momentum, last = pl.pallas_call(
            functools.partial(exchange, group, waves),
            name="update",
            out_shape=(block, block, fifth),
            in_specs=[in_hbm] * 3,
            out_specs=[in_vmem] * 3,
            scratch_shapes=[
                pltpu.VMEM(g.shape, f32),
                pltpu.VMEM(g.shape, f32),
                blocks,
                blocks,
                blocks,
                pltpu.VMEM((side, wide), f32),
                squares,
                squares,
                sem((2, waves)),
                sem,
                sem((waves,)),
                sem((waves,)),
                sem((waves,)),
                sem((waves,)),
                sem((waves,)),
                sem((waves,)),
            ],
            compiler_params=pltpu.CompilerParams(
                collective_id=0, has_side_effects=True, vmem_limit_bytes=48 * MIB
            ),
        )(g, m, w)
        return pl.pallas_call(
            store,
            name="store",
            out_shape=(block, block),
            in_specs=[in_vmem] * 3,
            out_specs=[in_hbm] * 2,
            scratch_shapes=[pltpu.VMEM(fifth.shape, f32), sem((3,))],
            compiler_params=pltpu.CompilerParams(vmem_limit_bytes=16 * MIB),
        )(weights, momentum, last)

    specs = P("shift", "fsdp", "tp")
    return jax.shard_map(
        body, mesh=mesh, in_specs=(specs,) * 3, out_specs=(specs,) * 2, check_vma=False
    )
```

time: 108 us -> 105 us (0.972)
  the two profiles are of different devices: /device:TPU:1 before, /device:TPU:32 now
where the time goes in v3:
time: 105 us; the launch traced here: 104 us
  Pallas kernels  103 us (98%)
    pallas_call x1, Pallas kernels, body(): pl.pallas_call(functools.partial(exchange, group, waves), name='update',...  101 us

profile of v3, /device:TPU:32, one launch (start us, length us, event | category | flops | bytes accessed | tf_op | source)
XLA Modules:
  0.0 104.0 jit_solution(3166718543109715987)
XLA Ops:
  0.6 101.3 %update.1 = (f32[128,4,1024]{2,1,0:T(4,128)S(1)}, f32[128,4,1024]{2,1,0:T(4,128)S(1)}, f32[32,4,1024]{2,1,0:T(4,128)S(1)}) custom-call(f32[128,4,1024]{2,1,0:T(4,128)} %g_ref.1, f32[128,4,1024]{2,1,0:T(4,128)} %m_ref.1, f32[128,4,1024]{2,1,0:T(4,128)} %w_ref.1), custom_call_target="tpu_custom_call" | custom-call | tf_op jit(solution)/shard_map/update/pallas_call | solution.py:237
  102.0 2.0 %store.1 = (f32[128,4,1024]{2,1,0:T(4,128)}, f32[128,4,1024]{2,1,0:T(4,128)}) custom-call(f32[128,4,1024]{2,1,0:T(4,128)S(1)} %get-tuple-element.5.weights, f32[128,4,1024]{2,1,0:T(4,128)S(1)} %get-tuple-element.6.momentum, f32[32,4,1024]{2,1,0:T(4,128)S(1)} %get-tuple-element.7.last), custom_call_target="tpu_custom_call" | custom-call | tf_op jit(solution)/shard_map/store/pallas_call | solution.py:265

commit v4 on v3

--- a/solution.py
+++ b/solution.py
@@ -61,12 +61,11 @@
     w_ref,
     weights,
     momentum,
-    last,
+    returned,
     g_buf,
     m_buf,
     arrived,
     leaving,
-    returned,
     rows,
     gram_out,
     gram_in,
@@ -78,6 +77,8 @@
     gram_recv,
     back_send,
     back_recv,
+    up_sem,
+    down_sem,
 ):
     me, half = lax.axis_index("fsdp"), lax.axis_index("tp")
     near, other = rows.shape[0] // group, lax.rem(half + 1, 2)
@@ -90,14 +91,15 @@
 
     barrier = pltpu.get_barrier_semaphore()
 
-    def greet(o, _):
+    close = [step for step in order() if step[0] in (0, 1, depth - 1)]
+    for step in close:
+        pl.semaphore_signal(barrier, inc=1, device_id={"fsdp": partner(step)}, device_id_type=MESH)
+    pl.semaphore_signal(barrier, inc=1, device_id={"tp": other}, device_id_type=MESH)
+
+    def tell(sem, dz):
         pl.semaphore_signal(
-            barrier, inc=1, device_id={"fsdp": lax.rem(me + o, group)}, device_id_type=MESH
-        )
-        return 0
-
-    lax.fori_loop(1, group, greet, 0)
-    pl.semaphore_signal(barrier, inc=1, device_id={"tp": other}, device_id_type=MESH)
+            sem, inc=1, device_id={"fsdp": partner((dz, 0, 0))}, device_id_type=MESH
+        )
 
     def part(w):
         return pl.ds(w * group, group)
@@ -151,19 +153,40 @@
             device_id_type=MESH,
         )
 
-    for w in range(waves):
+    def momenta(w):
         for copy in loads(w):
             copy.wait()
         momentum[part(w)] = hold_rate * m_buf[part(w)] + g_buf[part(w)]
         arrived[w, me] = momentum[w * group + me]
-    pl.semaphore_wait(barrier, group)
+
+    def first_out(*distances):
+        for step in order():
+            if step[0] in distances:
+                out_copy(0, partner(step)).start()
+
+    momenta(0)
+    pl.semaphore_wait(barrier, len(close) + 1)
+    tell(up_sem.at[0], 1)
+    tell(down_sem.at[0], depth - 1)
+    first_out(0, 1, depth - 1)
+    for hop in range(1, depth // 2):
+        momenta(hop)
+        pl.semaphore_wait(up_sem.at[hop - 1], 1)
+        if hop < depth // 2 - 1:
+            tell(up_sem.at[hop], 1)
+            pl.semaphore_wait(down_sem.at[hop - 1], 1)
+            if hop < depth // 2 - 2:
+                tell(down_sem.at[hop], depth - 1)
+            first_out(hop + 1, depth - hop - 1)
+        else:
+            first_out(hop + 1)
 
     def send_out(w, _):
         for step in order():
             out_copy(w, partner(step)).start()
         return 0
 
-    lax.fori_loop(0, waves, send_out, 0)
+    lax.fori_loop(1, waves, send_out, 0)
 
     def wave(w, _):
         all_of(arrived, w, out_send, out_recv).wait_recv()
@@ -179,8 +202,23 @@
         product = times(mix, rows[...])
         for k in range(group):
             leaving[w, k] = product[near * k : near * (k + 1)]
-        for step in order():
-            back_copy(w, partner(step)).start()
+        @pl.when(w < waves - 2)
+        def _():
+            for step in order():
+                back_copy(w, partner(step)).start()
+
+        @pl.when(w >= waves - 2)
+        def _():
+            for to_z in (0, 1, 2, 3, 7, 4, 6, 5):
+                for b, c in ((1, 1), (0, 1), (1, 0), (0, 0)):
+                    to = to_z * 4 + lax.rem(y + b, 2) * 2 + lax.rem(core + c, 2)
+                    if b or c:
+                        back_copy(w, to).start()
+                    else:
+                        @pl.when(to != me)
+                        def _(to=to):
+                            back_copy(w, to).start()
+
         returned[w, me] = leaving[w, me]
         return 0
 
@@ -202,20 +240,19 @@
 
     lax.fori_loop(0, waves, drain, 0)
     all_of(returned, waves - 1, back_send, back_recv).wait_recv()
-    last[...] = returned[waves - 1]
-
-
-def store(weights, momentum, last, weights_out, momentum_out, fresh, sem):
-    done = weights.shape[0] - last.shape[0]
-    tail = pl.ds(done, last.shape[0])
+
+
+def store(weights, momentum, returned, weights_out, momentum_out, fresh, sem):
+    waves, group = returned.shape[:2]
+    done, tail = pl.ds(0, (waves - 1) * group), pl.ds((waves - 1) * group, group)
     copies = [
-        pltpu.make_async_copy(weights.at[pl.ds(0, done)], weights_out.at[pl.ds(0, done)], sem.at[0]),
+        pltpu.make_async_copy(weights.at[done], weights_out.at[done], sem.at[0]),
         pltpu.make_async_copy(momentum, momentum_out, sem.at[1]),
         pltpu.make_async_copy(fresh, weights_out.at[tail], sem.at[2]),
     ]
     copies[0].start()
     copies[1].start()
-    fresh[...] = weights[tail] - learn_rate * last[...]
+    fresh[...] = weights[tail] - learn_rate * returned[waves - 1]
     copies[2].start()
     for copy in copies:
         copy.wait()
@@ -229,15 +266,15 @@
         waves, side = mats // group, near * group
         f32 = jnp.float32
         block = jax.ShapeDtypeStruct(g.shape, f32)
-        fifth = jax.ShapeDtypeStruct((group, near, wide), f32)
         sem = pltpu.SemaphoreType.DMA
         in_hbm, in_vmem = pl.BlockSpec(memory_space=pltpu.HBM), pl.BlockSpec(memory_space=pltpu.VMEM)
         blocks = pltpu.VMEM((waves, group, near, wide), f32)
+        split = jax.ShapeDtypeStruct(blocks.shape, f32)
         squares = pltpu.VMEM((waves, side, side), f32)
-        weights, momentum, last = pl.pallas_call(
+        weights, momentum, returned = pl.pallas_call(
             functools.partial(exchange, group, waves),
             name="update",
-            out_shape=(block, block, fifth),
+            out_shape=(block, block, split),
             in_specs=[in_hbm] * 3,
             out_specs=[in_vmem] * 3,
             scratch_shapes=[
@@ -245,7 +282,6 @@
                 pltpu.VMEM(g.shape, f32),
                 blocks,
                 blocks,
-                blocks,
                 pltpu.VMEM((side, wide), f32),
                 squares,
                 squares,
@@ -257,9 +293,11 @@
                 sem((waves,)),
                 sem((waves,)),
                 sem((waves,)),
+                pltpu.SemaphoreType.REGULAR((group // 8 - 1,)),
+                pltpu.SemaphoreType.REGULAR((group // 8 - 2,)),
             ],
             compiler_params=pltpu.CompilerParams(
-                collective_id=0, has_side_effects=True, vmem_limit_bytes=48 * MIB
+                collective_id=0, has_side_effects=True, vmem_limit_bytes=46 * MIB
             ),
         )(g, m, w)
         return pl.pallas_call(
@@ -268,9 +306,9 @@
             out_shape=(block, block),
             in_specs=[in_vmem] * 3,
             out_specs=[in_hbm] * 2,
-            scratch_shapes=[pltpu.VMEM(fifth.shape, f32), sem((3,))],
+            scratch_shapes=[pltpu.VMEM((group, near, wide), f32), sem((3,))],
             compiler_params=pltpu.CompilerParams(vmem_limit_bytes=16 * MIB),
-        )(weights, momentum, last)
+        )(weights, momentum, returned)
 
     specs = P("shift", "fsdp", "tp")
     return jax.shard_map(

time: 105 us -> 102 us (0.971)
  Pallas kernels: 103 us -> 101 us
    pallas_call x1, Pallas kernels: 101 us -> 99.1 us  [body(): pl.pallas_call(functools.partial(exchange, group, waves), name='update',...]
where the time goes in v4:
time: 102 us
  Pallas kernels  101 us (99%)
    pallas_call x1, Pallas kernels, body(): pl.pallas_call(functools.partial(exchange, group, waves), name='update',...  99.1 us

profile of v4, /device:TPU:32, one launch (start us, length us, event | category | flops | bytes accessed | tf_op | source)
XLA Modules:
  0.0 101.8 jit_solution(8947739511283797233)
XLA Ops:
  0.6 99.1 %update.1 = (f32[128,4,1024]{2,1,0:T(4,128)S(1)}, f32[128,4,1024]{2,1,0:T(4,128)S(1)}, f32[4,32,4,1024]{3,2,1,0:T(4,128)S(1)}) custom-call(f32[128,4,1024]{2,1,0:T(4,128)} %g_ref.1, f32[128,4,1024]{2,1,0:T(4,128)} %m_ref.1, f32[128,4,1024]{2,1,0:T(4,128)} %w_ref.1), custom_call_target="tpu_custom_call" | custom-call | tf_op jit(solution)/shard_map/update/pallas_call | solution.py:274
  99.8 2.0 %store.1 = (f32[128,4,1024]{2,1,0:T(4,128)}, f32[128,4,1024]{2,1,0:T(4,128)}) custom-call(f32[128,4,1024]{2,1,0:T(4,128)S(1)} %get-tuple-element.5.weights, f32[128,4,1024]{2,1,0:T(4,128)S(1)} %get-tuple-element.6.momentum, f32[4,32,4,1024]{3,2,1,0:T(4,128)S(1)} %get-tuple-element.7.returned), custom_call_target="tpu_custom_call" | custom-call | tf_op jit(solution)/shard_map/store/pallas_call | solution.py:303

commit v5 on v4

--- a/solution.py
+++ b/solution.py
@@ -13,16 +13,12 @@
 hold_rate = 0.95
 learn_rate = 0.9
 
+CORNERS = ((1, 1), (0, 1), (1, 0), (0, 0))
+
+
 def order():
-    plus = [(dz, b, c) for b, c in ((0, 0), (1, 1), (0, 1), (1, 0)) for dz in (3, 2, 1)]
-    minus = [(dz, b, c) for b, c in ((0, 0), (1, 1), (0, 1), (1, 0)) for dz in (5, 6, 7)]
-    far = [(4, b, c) for b, c in ((0, 0), (1, 1), (0, 1), (1, 0))]
-    out = []
-    for i, pair in enumerate(zip(plus, minus)):
-        out += pair
-        if i % 3 == 2:
-            out.append(far[i // 3])
-    return out + [(0, 1, 0), (0, 0, 1), (0, 1, 1)]
+    steps = [(dz, b, c) for dz in (5, 4, 3, 6, 2, 7, 1, 0) for b, c in CORNERS]
+    return [step for step in steps if any(step)]
 
 
 def full_dot(a, b, dims):
@@ -79,6 +75,7 @@
     back_recv,
     up_sem,
     down_sem,
+    side_sem,
 ):
     me, half = lax.axis_index("fsdp"), lax.axis_index("tp")
     near, other = rows.shape[0] // group, lax.rem(half + 1, 2)
@@ -87,22 +84,13 @@
 
     def partner(step):
         dz, dy, dc = step
-        return lax.rem(z + dz, depth) * 4 + lax.rem(y + dy, 2) * 2 + lax.rem(core + dc, 2)
-
-    barrier = pltpu.get_barrier_semaphore()
-
-    close = [step for step in order() if step[0] in (0, 1, depth - 1)]
-    for step in close:
-        pl.semaphore_signal(barrier, inc=1, device_id={"fsdp": partner(step)}, device_id_type=MESH)
-    pl.semaphore_signal(barrier, inc=1, device_id={"tp": other}, device_id_type=MESH)
-
-    def tell(sem, dz):
-        pl.semaphore_signal(
-            sem, inc=1, device_id={"fsdp": partner((dz, 0, 0))}, device_id_type=MESH
-        )
+        turned = lax.rem(z, 2) * (depth - 2 * dz)
+        return lax.rem(z + dz + turned, depth) * 4 + lax.rem(y + dy, 2) * 2 + lax.rem(core + dc, 2)
 
     def part(w):
         return pl.ds(w * group, group)
+
+    barrier = pltpu.get_barrier_semaphore()
 
     def loads(w):
         return (
@@ -110,9 +98,22 @@
             pltpu.make_async_copy(m_ref.at[part(w)], m_buf.at[part(w)], load_sem.at[1, w]),
         )
 
-    for w in range(waves):
+    for copy in loads(0):
+        copy.start()
+    close = [s for s in order() if s[0] == 0 or s[0] in (1, depth - 1) and s[1] == 0]
+    close.sort(key=lambda s: s[0] == 0)
+    beside = {"fsdp": partner((0, 1, 0)), "tp": other}
+    for step in close:
+        pl.semaphore_signal(barrier, inc=1, device_id={"fsdp": partner(step)}, device_id_type=MESH)
+    pl.semaphore_signal(barrier, inc=1, device_id=beside, device_id_type=MESH)
+    for w in range(1, waves):
         for copy in loads(w):
             copy.start()
+
+    def tell(sem, dz):
+        to = lax.rem(me + 4 * dz, group)
+        pl.semaphore_signal(sem, inc=1, device_id={"fsdp": to}, device_id_type=MESH)
+
     w_copy = pltpu.make_async_copy(w_ref, weights, w_sem)
     w_copy.start()
 
@@ -159,27 +160,30 @@
         momentum[part(w)] = hold_rate * m_buf[part(w)] + g_buf[part(w)]
         arrived[w, me] = momentum[w * group + me]
 
-    def first_out(*distances):
-        for step in order():
-            if step[0] in distances:
-                out_copy(0, partner(step)).start()
-
+    def first_out(hop):
+        for dz, b, c in sorted(order(), key=lambda s: s[0] == 0):
+            hops = min(dz, depth - dz)
+            if hops == hop + 1 - b or hops == hop == 0:
+                out_copy(0, partner((dz, b, c))).start()
+
+    far = depth // 2
     momenta(0)
     pl.semaphore_wait(barrier, len(close) + 1)
     tell(up_sem.at[0], 1)
     tell(down_sem.at[0], depth - 1)
-    first_out(0, 1, depth - 1)
-    for hop in range(1, depth // 2):
-        momenta(hop)
+    first_out(0)
+    pl.semaphore_signal(side_sem, inc=1, device_id=beside, device_id_type=MESH)
+    for hop in range(1, far + 1):
+        if hop < waves:
+            momenta(hop)
         pl.semaphore_wait(up_sem.at[hop - 1], 1)
-        if hop < depth // 2 - 1:
+        if hop < far:
             tell(up_sem.at[hop], 1)
             pl.semaphore_wait(down_sem.at[hop - 1], 1)
-            if hop < depth // 2 - 2:
+            if hop < far - 1:
                 tell(down_sem.at[hop], depth - 1)
-            first_out(hop + 1, depth - hop - 1)
-        else:
-            first_out(hop + 1)
+        first_out(hop)
+    pl.semaphore_wait(side_sem, 1)
 
     def send_out(w, _):
         for step in order():
@@ -209,15 +213,20 @@
 
         @pl.when(w >= waves - 2)
         def _():
-            for to_z in (0, 1, 2, 3, 7, 4, 6, 5):
-                for b, c in ((1, 1), (0, 1), (1, 0), (0, 0)):
+            for to_z in (0,):
+                for b, c in CORNERS:
                     to = to_z * 4 + lax.rem(y + b, 2) * 2 + lax.rem(core + c, 2)
-                    if b or c:
+
+                    @pl.when(to != me)
+                    def _(to=to):
                         back_copy(w, to).start()
-                    else:
-                        @pl.when(to != me)
-                        def _(to=to):
-                            back_copy(w, to).start()
+
+            for step in order():
+                to = partner(step)
+
+                @pl.when(to >= 4)
+                def _(to=to):
+                    back_copy(w, to).start()
 
         returned[w, me] = leaving[w, me]
         return 0
@@ -293,8 +302,9 @@
                 sem((waves,)),
                 sem((waves,)),
                 sem((waves,)),
+                pltpu.SemaphoreType.REGULAR((group // 8,)),
                 pltpu.SemaphoreType.REGULAR((group // 8 - 1,)),
-                pltpu.SemaphoreType.REGULAR((group // 8 - 2,)),
+                pltpu.SemaphoreType.REGULAR,
             ],
             compiler_params=pltpu.CompilerParams(
                 collective_id=0, has_side_effects=True, vmem_limit_bytes=46 * MIB

time: 102 us -> 102 us (level)
  no operation moved by 1% of the time
where the time goes in v5:
time: 102 us
  Pallas kernels  101 us (99%)
    pallas_call x1, Pallas kernels, body(): pl.pallas_call(functools.partial(exchange, group, waves), name='update',...  99.3 us

profile of v5, /device:TPU:32, one launch (start us, length us, event | category | flops | bytes accessed | tf_op | source)
XLA Modules:
  0.0 101.9 jit_solution(17693865884434770788)
XLA Ops:
  0.6 99.3 %update.1 = (f32[128,4,1024]{2,1,0:T(4,128)S(1)}, f32[128,4,1024]{2,1,0:T(4,128)S(1)}, f32[4,32,4,1024]{3,2,1,0:T(4,128)S(1)}) custom-call(f32[128,4,1024]{2,1,0:T(4,128)} %g_ref.1, f32[128,4,1024]{2,1,0:T(4,128)} %m_ref.1, f32[128,4,1024]{2,1,0:T(4,128)} %w_ref.1), custom_call_target="tpu_custom_call" | custom-call | tf_op jit(solution)/shard_map/update/pallas_call | solution.py:283
  99.9 2.0 %store.1 = (f32[128,4,1024]{2,1,0:T(4,128)}, f32[128,4,1024]{2,1,0:T(4,128)}) custom-call(f32[128,4,1024]{2,1,0:T(4,128)S(1)} %get-tuple-element.5.weights, f32[128,4,1024]{2,1,0:T(4,128)S(1)} %get-tuple-element.6.momentum, f32[4,32,4,1024]{3,2,1,0:T(4,128)S(1)} %get-tuple-element.7.returned), custom_call_target="tpu_custom_call" | custom-call | tf_op jit(solution)/shard_map/store/pallas_call | solution.py:313

commit v6 on v5

--- a/solution.py
+++ b/solution.py
@@ -206,27 +206,22 @@
         product = times(mix, rows[...])
         for k in range(group):
             leaving[w, k] = product[near * k : near * (k + 1)]
-        @pl.when(w < waves - 2)
+        @pl.when(w < waves - 1)
         def _():
             for step in order():
                 back_copy(w, partner(step)).start()
 
-        @pl.when(w >= waves - 2)
+        @pl.when(w >= waves - 1)
         def _():
-            for to_z in (0,):
+            for to_z in (0, 1, 2, 3, 7, 4, 6, 5):
                 for b, c in CORNERS:
                     to = to_z * 4 + lax.rem(y + b, 2) * 2 + lax.rem(core + c, 2)
-
-                    @pl.when(to != me)
-                    def _(to=to):
+                    if b or c:
                         back_copy(w, to).start()
-
-            for step in order():
-                to = partner(step)
-
-                @pl.when(to >= 4)
-                def _(to=to):
-                    back_copy(w, to).start()
+                    else:
+                        @pl.when(to != me)
+                        def _(to=to):
+                            back_copy(w, to).start()
 
         returned[w, me] = leaving[w, me]
         return 0

time: 102 us -> 102 us (level); the launches traced: 102 us -> 101 us
    pallas_call x1, Pallas kernels: 99.3 us -> 98.1 us  [body(): pl.pallas_call(functools.partial(exchange, group, waves), name='update',...]
where the time goes in v6:
time: 102 us; the launch traced here: 101 us
  Pallas kernels  100 us (98%)
    pallas_call x1, Pallas kernels, body(): pl.pallas_call(functools.partial(exchange, group, waves), name='update',...  98.1 us

profile of v6, /device:TPU:32, one launch (start us, length us, event | category | flops | bytes accessed | tf_op | source)
XLA Modules:
  0.0 100.8 jit_solution(9081201349943652434)
XLA Ops:
  0.6 98.1 %update.1 = (f32[128,4,1024]{2,1,0:T(4,128)S(1)}, f32[128,4,1024]{2,1,0:T(4,128)S(1)}, f32[4,32,4,1024]{3,2,1,0:T(4,128)S(1)}) custom-call(f32[128,4,1024]{2,1,0:T(4,128)} %g_ref.1, f32[128,4,1024]{2,1,0:T(4,128)} %m_ref.1, f32[128,4,1024]{2,1,0:T(4,128)} %w_ref.1), custom_call_target="tpu_custom_call" | custom-call | tf_op jit(solution)/shard_map/update/pallas_call | solution.py:278
  98.8 2.0 %store.1 = (f32[128,4,1024]{2,1,0:T(4,128)}, f32[128,4,1024]{2,1,0:T(4,128)}) custom-call(f32[128,4,1024]{2,1,0:T(4,128)S(1)} %get-tuple-element.5.weights, f32[128,4,1024]{2,1,0:T(4,128)S(1)} %get-tuple-element.6.momentum, f32[4,32,4,1024]{3,2,1,0:T(4,128)S(1)} %get-tuple-element.7.returned), custom_call_target="tpu_custom_call" | custom-call | tf_op jit(solution)/shard_map/store/pallas_call | solution.py:308

commit v7 on v6

--- a/solution.py
+++ b/solution.py
@@ -174,8 +174,6 @@
     first_out(0)
     pl.semaphore_signal(side_sem, inc=1, device_id=beside, device_id_type=MESH)
     for hop in range(1, far + 1):
-        if hop < waves:
-            momenta(hop)
         pl.semaphore_wait(up_sem.at[hop - 1], 1)
         if hop < far:
             tell(up_sem.at[hop], 1)
@@ -183,6 +181,8 @@
             if hop < far - 1:
                 tell(down_sem.at[hop], depth - 1)
         first_out(hop)
+    for w in range(1, waves):
+        momenta(w)
     pl.semaphore_wait(side_sem, 1)
 
     def send_out(w, _):
@@ -246,20 +246,59 @@
     all_of(returned, waves - 1, back_send, back_recv).wait_recv()
 
 
-def store(weights, momentum, returned, weights_out, momentum_out, fresh, sem):
+def is_early():
+    return lax.axis_index("fsdp") < 12
+
+
+def store_early(g_ref, m_ref, momentum_out, g_buf, m_buf, sem):
+    @pl.when(is_early())
+    def _():
+        parts = [pl.ds(32 * i, 32) for i in range(g_buf.shape[0] // 32)]
+        loads = [
+            (
+                pltpu.make_async_copy(g_ref.at[part], g_buf.at[part], sem.at[0, i]),
+                pltpu.make_async_copy(m_ref.at[part], m_buf.at[part], sem.at[1, i]),
+            )
+            for i, part in enumerate(parts)
+        ]
+        stores = [
+            pltpu.make_async_copy(g_buf.at[part], momentum_out.at[part], sem.at[2, i])
+            for i, part in enumerate(parts)
+        ]
+        for pair in loads:
+            for copy in pair:
+                copy.start()
+        for part, pair, copy in zip(parts, loads, stores):
+            for load in pair:
+                load.wait()
+            g_buf[part] = hold_rate * m_buf[part] + g_buf[part]
+            copy.start()
+        for copy in stores:
+            copy.wait()
+
+
+def store(weights, momentum, returned, begun, weights_out, momentum_out, fresh, sem):
     waves, group = returned.shape[:2]
     done, tail = pl.ds(0, (waves - 1) * group), pl.ds((waves - 1) * group, group)
     copies = [
         pltpu.make_async_copy(weights.at[done], weights_out.at[done], sem.at[0]),
-        pltpu.make_async_copy(momentum, momentum_out, sem.at[1]),
-        pltpu.make_async_copy(fresh, weights_out.at[tail], sem.at[2]),
+        pltpu.make_async_copy(fresh, weights_out.at[tail], sem.at[1]),
     ]
+    other = pltpu.make_async_copy(momentum, momentum_out, sem.at[2])
     copies[0].start()
+
+    @pl.when(jnp.logical_not(is_early()))
+    def _():
+        other.start()
+
+    fresh[...] = weights[tail] - learn_rate * returned[waves - 1]
     copies[1].start()
-    fresh[...] = weights[tail] - learn_rate * returned[waves - 1]
-    copies[2].start()
     for copy in copies:
         copy.wait()
+
+    @pl.when(jnp.logical_not(is_early()))
+    def _():
+        other.wait()
 
 
 def solution(mesh):
@@ -275,6 +314,15 @@
         blocks = pltpu.VMEM((waves, group, near, wide), f32)
         split = jax.ShapeDtypeStruct(blocks.shape, f32)
         squares = pltpu.VMEM((waves, side, side), f32)
+        begun = pl.pallas_call(
+            store_early,
+            name="store_early",
+            out_shape=block,
+            in_specs=[in_hbm] * 2,
+            out_specs=in_hbm,
+            scratch_shapes=[pltpu.VMEM(g.shape, f32), pltpu.VMEM(g.shape, f32), sem((3, mats // 32))],
+            compiler_params=pltpu.CompilerParams(vmem_limit_bytes=60 * MIB, has_side_effects=True),
+        )(g, m)
         weights, momentum, returned = pl.pallas_call(
             functools.partial(exchange, group, waves),
             name="update",
@@ -309,11 +357,12 @@
             store,
             name="store",
             out_shape=(block, block),
-            in_specs=[in_vmem] * 3,
+            in_specs=[in_vmem] * 3 + [in_hbm],
             out_specs=[in_hbm] * 2,
+            input_output_aliases={3: 1},
             scratch_shapes=[pltpu.VMEM((group, near, wide), f32), sem((3,))],
             compiler_params=pltpu.CompilerParams(vmem_limit_bytes=16 * MIB),
-        )(weights, momentum, returned)
+        )(weights, momentum, returned, begun)
 
     specs = P("shift", "fsdp", "tp")
     return jax.shard_map(

time: 102 us -> 102 us (level)
    pallas_call x0 -> x1, Pallas kernels: none -> 3.12 us  [body(): pl.pallas_call(store_early, name='store_early', out_shape=block, in_specs...]
    pallas_call x1, Pallas kernels: 98.1 us -> 95.4 us  [body(): pl.pallas_call(functools.partial(exchange, group, waves), name='update',...]
where the time goes in v7:
time: 102 us; the launch traced here: 100 us
  Pallas kernels  99.8 us (98%)
    pallas_call x1, Pallas kernels, body(): pl.pallas_call(functools.partial(exchange, group, waves), name='update',...  95.4 us
    pallas_call x1, Pallas kernels, body(): pl.pallas_call(store_early, name='store_early', out_shape=block, in_specs...  3.12 us

profile of v7, /device:TPU:32, one launch (start us, length us, event | category | flops | bytes accessed | tf_op | source)
XLA Modules:
  0.0 100.5 jit_solution(11136534254933650904)
XLA Ops:
  0.6 3.1 %store_early.1.begun = f32[128,4,1024]{2,1,0:T(4,128)} custom-call(f32[128,4,1024]{2,1,0:T(4,128)} %g_ref.3, f32[128,4,1024]{2,1,0:T(4,128)} %m_ref.3), custom_call_target="tpu_custom_call" | custom-call | tf_op jit(solution)/shard_map/store_early/pallas_call | solution.py:317
  3.8 95.4 %update.1 = (f32[128,4,1024]{2,1,0:T(4,128)S(1)}, f32[128,4,1024]{2,1,0:T(4,128)S(1)}, f32[4,32,4,1024]{3,2,1,0:T(4,128)S(1)}) custom-call(f32[128,4,1024]{2,1,0:T(4,128)} %g_ref.3, f32[128,4,1024]{2,1,0:T(4,128)} %m_ref.3, f32[128,4,1024]{2,1,0:T(4,128)} %w_ref.1), custom_call_target="tpu_custom_call" | custom-call | tf_op jit(solution)/shard_map/update/pallas_call | solution.py:326
  99.1 1.3 %store.1 = (f32[128,4,1024]{2,1,0:T(4,128)}, f32[128,4,1024]{2,1,0:T(4,128)}) custom-call(f32[128,4,1024]{2,1,0:T(4,128)S(1)} %get-tuple-element.5.weights, f32[128,4,1024]{2,1,0:T(4,128)S(1)} %get-tuple-element.6.momentum, f32[4,32,4,1024]{3,2,1,0:T(4,128)S(1)} %get-tuple-element.7.returned, ...), custom_call_target="tpu_custom_call", output_to_operand_aliasing={{1}: (3, {})} | custom-call | tf_op jit(solution)/shard_map/store/pallas_call | solution.py:356

commit v8 on v7

--- a/solution.py
+++ b/solution.py
@@ -106,16 +106,11 @@
     for step in close:
         pl.semaphore_signal(barrier, inc=1, device_id={"fsdp": partner(step)}, device_id_type=MESH)
     pl.semaphore_signal(barrier, inc=1, device_id=beside, device_id_type=MESH)
-    for w in range(1, waves):
-        for copy in loads(w):
-            copy.start()
-
     def tell(sem, dz):
         to = lax.rem(me + 4 * dz, group)
         pl.semaphore_signal(sem, inc=1, device_id={"fsdp": to}, device_id_type=MESH)
 
     w_copy = pltpu.make_async_copy(w_ref, weights, w_sem)
-    w_copy.start()
 
     def out_copy(w, to):
         return pltpu.make_async_remote_copy(
@@ -157,6 +152,10 @@
     def momenta(w):
         for copy in loads(w):
             copy.wait()
+        if w == 0:
+            for later in range(1, waves):
+                for copy in loads(later):
+                    copy.start()
         momentum[part(w)] = hold_rate * m_buf[part(w)] + g_buf[part(w)]
         arrived[w, me] = momentum[w * group + me]
 
@@ -191,6 +190,7 @@
         return 0
 
     lax.fori_loop(1, waves, send_out, 0)
+    w_copy.start()
 
     def wave(w, _):
         all_of(arrived, w, out_send, out_recv).wait_recv()

time: 102 us -> 102 us (level)
  no operation moved by 1% of the time
where the time goes in v8:
time: 102 us; the launch traced here: 101 us
  Pallas kernels  99.9 us (98%)
    pallas_call x1, Pallas kernels, body(): pl.pallas_call(functools.partial(exchange, group, waves), name='update',...  95.5 us
    pallas_call x1, Pallas kernels, body(): pl.pallas_call(store_early, name='store_early', out_shape=block, in_specs...  3.12 us

profile of v8, /device:TPU:32, one launch (start us, length us, event | category | flops | bytes accessed | tf_op | source)
XLA Modules:
  0.0 100.6 jit_solution(1376644253806775986)
XLA Ops:
  0.6 3.1 %store_early.1.begun = f32[128,4,1024]{2,1,0:T(4,128)} custom-call(f32[128,4,1024]{2,1,0:T(4,128)} %g_ref.3, f32[128,4,1024]{2,1,0:T(4,128)} %m_ref.3), custom_call_target="tpu_custom_call" | custom-call | tf_op jit(solution)/shard_map/store_early/pallas_call | solution.py:317
  3.8 95.5 %update.1 = (f32[128,4,1024]{2,1,0:T(4,128)S(1)}, f32[128,4,1024]{2,1,0:T(4,128)S(1)}, f32[4,32,4,1024]{3,2,1,0:T(4,128)S(1)}) custom-call(f32[128,4,1024]{2,1,0:T(4,128)} %g_ref.3, f32[128,4,1024]{2,1,0:T(4,128)} %m_ref.3, f32[128,4,1024]{2,1,0:T(4,128)} %w_ref.1), custom_call_target="tpu_custom_call" | custom-call | tf_op jit(solution)/shard_map/update/pallas_call | solution.py:326
  99.3 1.3 %store.1 = (f32[128,4,1024]{2,1,0:T(4,128)}, f32[128,4,1024]{2,1,0:T(4,128)}) custom-call(f32[128,4,1024]{2,1,0:T(4,128)S(1)} %get-tuple-element.5.weights, f32[128,4,1024]{2,1,0:T(4,128)S(1)} %get-tuple-element.6.momentum, f32[4,32,4,1024]{3,2,1,0:T(4,128)S(1)} %get-tuple-element.7.returned, ...), custom_call_target="tpu_custom_call", output_to_operand_aliasing={{1}: (3, {})} | custom-call | tf_op jit(solution)/shard_map/store/pallas_call | solution.py:356

commit v9 on v7

--- a/solution.py
+++ b/solution.py
@@ -213,7 +213,7 @@
 
         @pl.when(w >= waves - 1)
         def _():
-            for to_z in (0, 1, 2, 3, 7, 4, 6, 5):
+            for to_z in (0, 1, 2, 7, 3, 4, 6, 5):
                 for b, c in CORNERS:
                     to = to_z * 4 + lax.rem(y + b, 2) * 2 + lax.rem(core + c, 2)
                     if b or c:

time: 102 us -> 102 us (level)
  no operation moved by 1% of the time
where the time goes in v9:
time: 102 us; the launch traced here: 100 us
  Pallas kernels  99.8 us (98%)
    pallas_call x1, Pallas kernels, body(): pl.pallas_call(functools.partial(exchange, group, waves), name='update',...  95.4 us
    pallas_call x1, Pallas kernels, body(): pl.pallas_call(store_early, name='store_early', out_shape=block, in_specs...  3.12 us

profile of v9, /device:TPU:32, one launch (start us, length us, event | category | flops | bytes accessed | tf_op | source)
XLA Modules:
  0.0 100.5 jit_solution(2942017304584233903)
XLA Ops:
  0.6 3.1 %store_early.1.begun = f32[128,4,1024]{2,1,0:T(4,128)} custom-call(f32[128,4,1024]{2,1,0:T(4,128)} %g_ref.3, f32[128,4,1024]{2,1,0:T(4,128)} %m_ref.3), custom_call_target="tpu_custom_call" | custom-call | tf_op jit(solution)/shard_map/store_early/pallas_call | solution.py:317
  3.8 95.4 %update.1 = (f32[128,4,1024]{2,1,0:T(4,128)S(1)}, f32[128,4,1024]{2,1,0:T(4,128)S(1)}, f32[4,32,4,1024]{3,2,1,0:T(4,128)S(1)}) custom-call(f32[128,4,1024]{2,1,0:T(4,128)} %g_ref.3, f32[128,4,1024]{2,1,0:T(4,128)} %m_ref.3, f32[128,4,1024]{2,1,0:T(4,128)} %w_ref.1), custom_call_target="tpu_custom_call" | custom-call | tf_op jit(solution)/shard_map/update/pallas_call | solution.py:326
  99.1 1.3 %store.1 = (f32[128,4,1024]{2,1,0:T(4,128)}, f32[128,4,1024]{2,1,0:T(4,128)}) custom-call(f32[128,4,1024]{2,1,0:T(4,128)S(1)} %get-tuple-element.5.weights, f32[128,4,1024]{2,1,0:T(4,128)S(1)} %get-tuple-element.6.momentum, f32[4,32,4,1024]{3,2,1,0:T(4,128)S(1)} %get-tuple-element.7.returned, ...), custom_call_target="tpu_custom_call", output_to_operand_aliasing={{1}: (3, {})} | custom-call | tf_op jit(solution)/shard_map/store/pallas_call | solution.py:356
